TPU v7x, 8 devices: a whole 2x2x1 slice. The times are simulated.
8 devices in a mesh: data: 2 (over z, y), dap: 4 (over x, core).
Axes of the slice: x: 2, y: 2, z: 1, core: 2. Of those that a mesh axis runs over, the one named last changes fastest.
Arguments:
- z_one: bfloat16 [1024, 512, 128], P(('data', 'dap')), parts along dimension 0
- mask_one: int32 [1024, 512], P(('data', 'dap')), parts along dimension 0
- z_two: bfloat16 [1024, 512, 128], P(('data', 'dap')), parts along dimension 0
- mask_two: int32 [1024, 512], P(('data', 'dap')), parts along dimension 0
- norm_in: bfloat16 [2, 2, 128], replicated
- w_proj: bfloat16 [2, 128, 512], replicated
- w_gate: bfloat16 [2, 128, 128], replicated
- norm_mid: bfloat16 [2, 2, 128], replicated
- w_out: bfloat16 [2, 128, 128], replicated
Outputs:
- output 1: bfloat16 [1024, 512, 128], P(('data', 'dap')), parts along dimension 0
- output 2: bfloat16 [1024, 512, 128], P(('data', 'dap')), parts along dimension 0
There are 2 independent parts. A program takes and returns all parts, laid end to end along the dimension named above; an argument that names none is the same for every part.
All inputs are finite; a program needn't handle non-finite values.
Results may differ from a plain program's by a relative error of at most 0.00666387.
Values are sent between devices in bfloat16 or wider.
A program may use at most 1 GiB of HBM per device.

v0:
```python
import jax
import jax.numpy as jnp
from jax import lax
from jax.sharding import PartitionSpec as P


def layer_norm(vals, ln_gain, ln_shift, feature_axis):
    vals = vals.astype(jnp.float32)
    row_mean = jnp.mean(vals, axis=feature_axis, keepdims=True)
    centred = vals - row_mean
    row_var = jnp.mean(centred * centred, axis=feature_axis, keepdims=True)
    return centred * lax.rsqrt(row_var + 1e-5) * ln_gain.astype(jnp.float32) + ln_shift.astype(jnp.float32)


def project_rows(z_rows, mask_rows, norm_in, w_proj):
    pair_width = z_rows.shape[2]
    hidden = w_proj.shape[1] // 4
    x_norm = layer_norm(z_rows, norm_in[0], norm_in[1], -1).astype(jnp.bfloat16)
    w_split = w_proj.reshape(pair_width, 2, 2, hidden)
    projected = jnp.einsum("rnz,zsgc->sgcrn", x_norm, w_split, preferred_element_type=jnp.float32)
    keep_mask = mask_rows.astype(jnp.float32)
    sides = (keep_mask * jax.nn.sigmoid(projected[:, 1]) * projected[:, 0]).astype(jnp.bfloat16)
    return x_norm, sides


def finish_rows(z_rows, x_norm, t_rows, w_gate, norm_mid, w_out):
    t_norm = layer_norm(t_rows, norm_mid[0][:, None, None], norm_mid[1][:, None, None], 0).astype(jnp.bfloat16)
    update = jnp.einsum("crn,cz->rnz", t_norm, w_out, preferred_element_type=jnp.float32)
    gate_val = jax.nn.sigmoid(jnp.einsum("rnz,zy->rny", x_norm, w_gate, preferred_element_type=jnp.float32))
    return (z_rows.astype(jnp.float32) + gate_val * update).astype(jnp.bfloat16)


def tri_update(z_rows, mask_rows, norm_in, w_proj, w_gate, norm_mid, w_out, form):
    x_norm, sides = project_rows(z_rows, mask_rows, norm_in, w_proj)
    sides_chan = lax.all_to_all(sides, "dap", 1, 2, tiled=True)
    tri_prod = jnp.einsum(form, sides_chan[0], sides_chan[1], preferred_element_type=jnp.float32).astype(jnp.bfloat16)
    t_rows = lax.all_to_all(tri_prod, "dap", 1, 0, tiled=True)
    return finish_rows(z_rows, x_norm, t_rows, w_gate, norm_mid, w_out)


def solution(mesh):
    row_spec = P(("data", "dap"), None, None)
    mask_spec = P(("data", "dap"), None)
    replicated = P()

    def crop_update(z_rows, mask_rows, norm_in, w_proj, w_gate, norm_mid, w_out):
        z_mid = tri_update(z_rows, mask_rows, norm_in[0], w_proj[0], w_gate[0], norm_mid[0], w_out[0], "cik,cjk->cij")
        return tri_update(z_mid, mask_rows, norm_in[1], w_proj[1], w_gate[1], norm_mid[1], w_out[1], "cki,ckj->cij")

    def per_device(z_one, mask_one, z_two, mask_two, norm_in, w_proj, w_gate, norm_mid, w_out):
        return (crop_update(z_one, mask_one, norm_in, w_proj, w_gate, norm_mid, w_out),
                crop_update(z_two, mask_two, norm_in, w_proj, w_gate, norm_mid, w_out))

    return jax.shard_map(per_device, mesh=mesh,
                         in_specs=(row_spec, mask_spec, row_spec, mask_spec, replicated, replicated, replicated, replicated, replicated),
                         out_specs=(row_spec, row_spec), check_vma=False)
```

profile of v0, /device:TPU:0, one launch (start us, length us, event | category | flops | bytes accessed | tf_op | source)
XLA Modules:
  0.0 2991.0 jit_solution(7616958920317254472)
XLA Ops:
  0.7 22.5 copy.149
  39.2 50.9 %convolution_bitcast_fusion.3 = f32[2,2,128,128,512]{2,4,1,0,3:T(8,128)} fusion(bf16[128,2,2,128,1]{0,3,2,1,4:T(8,128)(2,1)S(1)} %bitcast.295, bf16[128,512,128]{1,2,0:T(8,128)(2,1)} %copy.149, f32[128]{0:T(128)S(1)} %get-tuple-element.29, f32[128]{0:T(128)S(1)} %get-tuple-element.30, f32[128,512]{1,0:T(8,128)S(1)} %add_rsqrt_fusion.7, ...), kind=kOutput, calls=%fused_computation.52 | convolution fusion | flops 8640266240 | bytes 151651328 | tf_op jit(solution)/shard_map/rnz,zsgc->sgcrn/dot_general | solution.py:20
  90.1 52.9 %fusion.22 = bf16[2,128,128,512]{1,3,0,2:T(8,128)(2,1)} fusion(f32[2,2,128,128,512]{2,4,1,0,3:T(8,128)} %convolution_bitcast_fusion.3, f32[128,512]{1,0:T(8,128)S(1)} %convert_element_type.206), kind=kLoop, calls=%fused_computation.29 | loop fusion | flops 100663296 | bytes 168034304 | tf_op jit(solution)/shard_map/convert_element_type | solution.py:22
  143.0 80.8 %copy.156 = bf16[2,128,128,512]{3,0,2,1:T(2,128)(2,1)} copy(bf16[2,128,128,512]{1,3,0,2:T(8,128)(2,1)} %fusion.22) | data formatting | bytes 67108864 | tf_op jit(solution)/shard_map/convert_element_type | solution.py:22
  233.7 22.4 copy.180
  270.9 50.9 %convolution_bitcast_fusion.1 = f32[2,2,128,128,512]{2,4,0,3,1:T(8,128)} fusion(bf16[128,2,2,128,1]{0,3,2,1,4:T(8,128)(2,1)S(1)} %bitcast.296, bf16[128,512,128]{1,2,0:T(8,128)(2,1)} %copy.180, f32[128,512]{1,0:T(8,128)S(1)} %add_rsqrt_fusion.3, f32[128,512]{1,0:T(8,128)S(1)} %broadcast_multiply_fusion.3, f32[128]{0:T(128)S(1)} %get-tuple-element.29, ...), kind=kOutput, calls=%fused_computation.38 | convolution fusion | flops 8640266240 | bytes 151651328 | tf_op jit(solution)/shard_map/rnz,zsgc->sgcrn/dot_general | solution.py:20
  321.8 52.9 %fusion.8 = bf16[2,128,128,512]{1,3,0,2:T(8,128)(2,1)} fusion(f32[2,2,128,128,512]{2,4,0,3,1:T(8,128)} %convolution_bitcast_fusion.1, f32[128,512]{1,0:T(8,128)S(1)} %convert_element_type.235), kind=kLoop, calls=%fused_computation.11 | loop fusion | flops 100663296 | bytes 168034304 | tf_op jit(solution)/shard_map/convert_element_type | solution.py:22
  374.6 80.9 %copy.185 = bf16[2,128,128,512]{3,0,2,1:T(2,128)(2,1)} copy(bf16[2,128,128,512]{1,3,0,2:T(8,128)(2,1)} %fusion.8) | data formatting | bytes 67108864 | tf_op jit(solution)/shard_map/convert_element_type | solution.py:22
  455.5 141.7 %all-to-all-done = bf16[2,128,128,512]{3,0,2,1:T(2,128)(2,1)} async-done(((bf16[2,128,128,512]{3,0,2,1:T(2,128)(2,1)}), bf16[2,128,128,512]{3,0,2,1:T(2,128)(2,1)}, u32[]{:S(2)}, u32[]{:S(2)}) %all-to-all-start) | async-done | bytes 33554464 | tf_op jit(solution)/shard_map/all_to_all | solution.py:35
  607.2 22.8 copy.157
  655.3 21.4 convolution_convert_fusion.3
  676.7 18.4 copy.160
  695.2 274.5 %all-to-all-done.4 = bf16[2,128,128,512]{3,0,2,1:T(2,128)(2,1)} async-done(((bf16[2,128,128,512]{3,0,2,1:T(2,128)(2,1)}), bf16[2,128,128,512]{3,0,2,1:T(2,128)(2,1)}, u32[]{:S(2)}, u32[]{:S(2)}) %all-to-all-start.4) | async-done | bytes 33554464 | tf_op jit(solution)/shard_map/all_to_all | solution.py:35
  976.7 23.0 copy.186
  1025.0 21.4 convolution_convert_fusion.1
  1046.5 18.5 copy.189
  1065.0 94.4 %all-to-all-done.1 = bf16[32,512,512]{2,0,1:T(8,128)(2,1)} async-done(((bf16[32,512,512]{2,0,1:T(8,128)(2,1)}), bf16[32,512,512]{2,0,1:T(8,128)(2,1)}, u32[]{:S(2)}, u32[]{:S(2)}) %all-to-all-start.1) | async-done | bytes 16777248 | tf_op jit(solution)/shard_map/all_to_all | solution.py:37
  1200.4 149.2 %all-to-all-done.5 = bf16[32,512,512]{2,0,1:T(8,128)(2,1)} async-done(((bf16[32,512,512]{2,0,1:T(8,128)(2,1)}), bf16[32,512,512]{2,0,1:T(8,128)(2,1)}, u32[]{:S(2)}, u32[]{:S(2)}) %all-to-all-start.5) | async-done | bytes 16777248 | tf_op jit(solution)/shard_map/all_to_all | solution.py:37
  1364.3 30.2 %fusion.72 = (bf16[4,32,128,512]{3,1,2,0:T(8,128)(2,1)}, bf16[4,32,128,512]{3,1,2,0:T(8,128)(2,1)}) fusion(f32[128,512]{1,0:T(8,128)S(1)} %add_rsqrt_fusion.2, f32[128,512]{1,0:T(8,128)S(1)} %broadcast_multiply_fusion.2, f32[4,32]{1,0:T(4,128)S(1)} %reshape.225, f32[4,32]{1,0:T(4,128)S(1)} %reshape.224, bf16[32,512,512]{2,0,1:T(8,128)(2,1)} %all-to-all-done.5, ...), kind=kLoop, calls=%fused_computation.98 | loop fusion | flops 100663296 | bytes 68158464 | tf_op jit(solution)/shard_map/convert_element_type | solution.py:27
  1408.6 29.6 convert_reduce_fusion.2
  1445.9 50.9 %convolution_bitcast_fusion.2 = f32[2,2,128,128,512]{2,4,0,3,1:T(8,128)} fusion(bf16[128,2,2,128,1]{0,3,2,1,4:T(8,128)(2,1)S(1)} %bitcast.293, bf16[128,512,128]{1,2,0:T(8,128)(2,1)} %get-tuple-element.35, f32[128]{0:T(128)S(1)} %copy-done.41, f32[128]{0:T(128)S(1)} %copy-done.38, f32[128,512]{1,0:T(8,128)S(1)} %add_rsqrt_fusion.5, ...), kind=kOutput, calls=%fused_computation.39 | convolution fusion | flops 8640266240 | bytes 151651328 | tf_op jit(solution)/shard_map/rnz,zsgc->sgcrn/dot_general | solution.py:20
  1496.8 52.9 %fusion.15 = bf16[2,128,128,512]{1,3,0,2:T(8,128)(2,1)} fusion(f32[2,2,128,128,512]{2,4,0,3,1:T(8,128)} %convolution_bitcast_fusion.2, f32[128,512]{1,0:T(8,128)S(1)} %copy-done.15), kind=kLoop, calls=%fused_computation.20 | loop fusion | flops 100663296 | bytes 168034304 | tf_op jit(solution)/shard_map/convert_element_type | solution.py:22
  1549.7 80.8 %copy.169 = bf16[2,128,128,512]{3,0,2,1:T(2,128)(2,1)} copy(bf16[2,128,128,512]{1,3,0,2:T(8,128)(2,1)} %fusion.15) | data formatting | bytes 67108864 | tf_op jit(solution)/shard_map/convert_element_type | solution.py:22
  1672.6 29.7 convert_reduce_fusion
  1710.0 50.9 %convolution_bitcast_fusion = f32[2,2,128,128,512]{2,4,0,3,1:T(8,128)} fusion(bf16[128,2,2,128,1]{0,3,2,1,4:T(8,128)(2,1)S(1)} %bitcast.294, bf16[128,512,128]{1,2,0:T(8,128)(2,1)} %get-tuple-element.33, f32[128,512]{1,0:T(8,128)S(1)} %add_rsqrt_fusion.1, f32[128,512]{1,0:T(8,128)S(1)} %broadcast_multiply_fusion.1, f32[128]{0:T(128)S(1)} %copy-done.42, ...), kind=kOutput, calls=%fused_computation.37 | convolution fusion | flops 8640266240 | bytes 151651328 | tf_op jit(solution)/shard_map/rnz,zsgc->sgcrn/dot_general | solution.py:20
  1760.9 52.9 %fusion.1 = bf16[2,128,128,512]{1,3,0,2:T(8,128)(2,1)} fusion(f32[2,2,128,128,512]{2,4,0,3,1:T(8,128)} %convolution_bitcast_fusion, f32[128,512]{1,0:T(8,128)S(1)} %copy-done.13), kind=kLoop, calls=%fused_computation.2 | loop fusion | flops 100663296 | bytes 168034304 | tf_op jit(solution)/shard_map/convert_element_type | solution.py:22
  1813.8 80.9 %copy.196 = bf16[2,128,128,512]{3,0,2,1:T(2,128)(2,1)} copy(bf16[2,128,128,512]{1,3,0,2:T(8,128)(2,1)} %fusion.1) | data formatting | bytes 67108864 | tf_op jit(solution)/shard_map/convert_element_type | solution.py:22
  1894.6 108.4 %all-to-all-done.2 = bf16[2,128,128,512]{3,0,2,1:T(2,128)(2,1)} async-done(((bf16[2,128,128,512]{3,0,2,1:T(2,128)(2,1)}), bf16[2,128,128,512]{3,0,2,1:T(2,128)(2,1)}, u32[]{:S(2)}, u32[]{:S(2)}) %all-to-all-start.2) | async-done | bytes 33554464 | tf_op jit(solution)/shard_map/all_to_all | solution.py:35
  2013.0 22.8 copy.170
  2035.7 23.0 fusion.128
  2058.7 26.1 copy.171
  2084.8 24.9 squeeze.39
  2123.7 21.9 convolution_convert_fusion.2
  2164.0 211.4 %all-to-all-done.6 = bf16[2,128,128,512]{3,0,2,1:T(2,128)(2,1)} async-done(((bf16[2,128,128,512]{3,0,2,1:T(2,128)(2,1)}), bf16[2,128,128,512]{3,0,2,1:T(2,128)(2,1)}, u32[]{:S(2)}, u32[]{:S(2)}) %all-to-all-start.6) | async-done | bytes 33554464 | tf_op jit(solution)/shard_map/all_to_all | solution.py:35
  2382.7 23.0 copy.197
  2405.7 23.0 fusion.126
  2428.7 26.1 copy.198
  2454.8 24.9 squeeze.86
  2493.6 21.9 convolution_convert_fusion
  2533.9 31.5 %all-to-all-done.3 = bf16[32,512,512]{2,0,1:T(8,128)(2,1)} async-done(((bf16[32,512,512]{2,0,1:T(8,128)(2,1)}), bf16[32,512,512]{2,0,1:T(8,128)(2,1)}, u32[]{:S(2)}, u32[]{:S(2)}) %all-to-all-start.3) | async-done | bytes 16777248 | tf_op jit(solution)/shard_map/all_to_all | solution.py:37
  2593.2 162.5 %all-to-all-done.7 = bf16[32,512,512]{2,0,1:T(8,128)(2,1)} async-done(((bf16[32,512,512]{2,0,1:T(8,128)(2,1)}), bf16[32,512,512]{2,0,1:T(8,128)(2,1)}, u32[]{:S(2)}, u32[]{:S(2)}) %all-to-all-start.7) | async-done | bytes 16777248 | tf_op jit(solution)/shard_map/all_to_all | solution.py:37
  2775.5 30.6 %fusion.64 = (bf16[4,32,128,512]{3,2,0,1:T(8,128)(2,1)}, bf16[4,32,128,512]{3,2,0,1:T(8,128)(2,1)}) fusion(f32[128,512]{1,0:T(8,128)S(1)} %add_rsqrt_fusion, f32[128,512]{1,0:T(8,128)S(1)} %broadcast_multiply_fusion, f32[4,32]{0,1:T(8,128)S(1)} %copy.176, f32[4,32]{0,1:T(8,128)S(1)} %copy.175, bf16[32,512,512]{2,0,1:T(8,128)(2,1)} %all-to-all-done.7, ...), kind=kLoop, calls=%fused_computation.89 | loop fusion | flops 100663296 | bytes 68158464 | tf_op jit(solution)/shard_map/convert_element_type | solution.py:27
  2820.1 25.1 fusion.93
  2845.2 30.6 %fusion.56 = bf16[128,512,128]{1,2,0:T(8,128)(2,1)} fusion(bf16[128,512,128]{1,2,0:T(8,128)(2,1)} %get-tuple-element.33, f32[128,512,128]{1,2,0:T(8,128)} %fusion.93, bf16[2,128,128]{2,1,0:T(8,128)(2,1)S(1)} %copy-done.37, f32[128,512]{1,0:T(8,128)S(1)} %copy-done.19, f32[128,512]{1,0:T(8,128)S(1)} %copy-done.9, f32[128]{0:T(128)S(1)} %copy-done.43, ...), kind=kOutput, calls=%fused_computation.80 | convolution fusion | flops 2256535552 | bytes 84444160 | tf_op jit(solution)/shard_map/rnz,zy->rny/dot_general | solution.py:29
  2875.8 22.4 copy.206
  2912.2 25.1 fusion.95
  2937.3 31.1 %fusion.54 = bf16[128,512,128]{1,2,0:T(8,128)(2,1)} fusion(bf16[128,512,128]{1,2,0:T(8,128)(2,1)} %get-tuple-element.35, f32[128,512,128]{1,2,0:T(8,128)} %fusion.95, bf16[2,128,128]{2,1,0:T(8,128)(2,1)S(1)} %copy-done.37, f32[128]{0:T(128)S(1)} %copy-done.43, f32[128]{0:T(128)S(1)} %copy-done.40, f32[128,512]{1,0:T(8,128)S(1)} %copy-done.17, ...), kind=kOutput, calls=%fused_computation.78 | convolution fusion | flops 2256535552 | bytes 84444160 | tf_op jit(solution)/shard_map/rnz,zy->rny/dot_general | solution.py:29
  2968.4 22.4 copy.205
  (165 shorter events, 392.7 us)
Async XLA Ops:
  0.6 37.1 %copy-start.44 = (bf16[2,2,128]{2,1,0:T(2,128)(2,1)S(1)}, bf16[2,2,128]{2,1,0:T(2,128)(2,1)}, u32[]{:S(2)}) copy-start(bf16[2,2,128]{2,1,0:T(2,128)(2,1)} %param.13) | copy-start | bytes 3076
  0.6 37.7 %copy-start.23 = (bf16[2,128,512]{2,1,0:T(8,128)(2,1)S(1)}, bf16[2,128,512]{2,1,0:T(8,128)(2,1)}, u32[]{:S(2)}) copy-start(bf16[2,128,512]{2,1,0:T(8,128)(2,1)} %param.14) | copy-start | bytes 786436
  0.7 38.5 %copy-start.24 = (s32[128,512]{1,0:T(8,128)S(1)}, s32[128,512]{1,0:T(8,128)}, u32[]{:S(2)}) copy-start(s32[128,512]{1,0:T(8,128)} %param.10) | copy-start | bytes 786436
  30.0 60.1 %copy-start.2 = (f32[128,512]{1,0:T(8,128)}, f32[128,512]{1,0:T(8,128)S(1)}, u32[]{:S(2)}) copy-start(f32[128,512]{1,0:T(8,128)S(1)} %broadcast_multiply_fusion.7) | copy-start | bytes 786436
  37.7 52.4 %copy-start.10 = (f32[128,512]{1,0:T(8,128)}, f32[128,512]{1,0:T(8,128)S(1)}, u32[]{:S(2)}) copy-start(f32[128,512]{1,0:T(8,128)S(1)} %add_rsqrt_fusion.7) | copy-start | bytes 786436
  38.4 232.5 %copy-start.26 = (f32[128]{0:T(128)}, f32[128]{0:T(128)S(1)}, u32[]{:S(2)}) copy-start(f32[128]{0:T(128)S(1)} %get-tuple-element.29) | copy-start | bytes 1540
  38.4 232.5 %copy-start.29 = (f32[128]{0:T(128)}, f32[128]{0:T(128)S(1)}, u32[]{:S(2)}) copy-start(f32[128]{0:T(128)S(1)} %get-tuple-element.30) | copy-start | bytes 1540
  39.2 50.9 %copy-start.14 = (f32[128,512]{1,0:T(8,128)}, f32[128,512]{1,0:T(8,128)S(1)}, u32[]{:S(2)}) copy-start(f32[128,512]{1,0:T(8,128)S(1)} %convert_element_type.206) | copy-start | bytes 786436
  223.8 373.4 %all-to-all-start = ((bf16[2,128,128,512]{3,0,2,1:T(2,128)(2,1)}), bf16[2,128,128,512]{3,0,2,1:T(2,128)(2,1)}, u32[]{:S(2)}, u32[]{:S(2)}) async-start(bf16[2,128,128,512]{3,0,2,1:T(2,128)(2,1)} %copy.156), calls=%async_computation | async-start | bytes 67108864 | tf_op jit(solution)/shard_map/all_to_all | solution.py:35
  256.2 65.6 %copy-start.12 = (f32[128,512]{1,0:T(8,128)}, f32[128,512]{1,0:T(8,128)S(1)}, u32[]{:S(2)}) copy-start(f32[128,512]{1,0:T(8,128)S(1)} %convert_element_type.235) | copy-start | bytes 786436
  263.2 58.6 %copy-start = (f32[128,512]{1,0:T(8,128)}, f32[128,512]{1,0:T(8,128)S(1)}, u32[]{:S(2)}) copy-start(f32[128,512]{1,0:T(8,128)S(1)} %broadcast_multiply_fusion.3) | copy-start | bytes 786436
  270.9 50.9 %copy-start.6 = (f32[128,512]{1,0:T(8,128)}, f32[128,512]{1,0:T(8,128)S(1)}, u32[]{:S(2)}) copy-start(f32[128,512]{1,0:T(8,128)S(1)} %add_rsqrt_fusion.3) | copy-start | bytes 786436
  597.2 372.4 %all-to-all-start.4 = ((bf16[2,128,128,512]{3,0,2,1:T(2,128)(2,1)}), bf16[2,128,128,512]{3,0,2,1:T(2,128)(2,1)}, u32[]{:S(2)}, u32[]{:S(2)}) async-start(bf16[2,128,128,512]{3,0,2,1:T(2,128)(2,1)} %copy.185), calls=%async_computation.4 | async-start | bytes 67108864 | tf_op jit(solution)/shard_map/all_to_all | solution.py:35
  969.6 189.7 %all-to-all-start.1 = ((bf16[32,512,512]{2,0,1:T(8,128)(2,1)}), bf16[32,512,512]{2,0,1:T(8,128)(2,1)}, u32[]{:S(2)}, u32[]{:S(2)}) async-start(bf16[32,512,512]{2,0,1:T(8,128)(2,1)} %copy.160), calls=%async_computation.1 | async-start | bytes 33554432 | tf_op jit(solution)/shard_map/all_to_all | solution.py:37
  1046.4 120.5 %copy-start.45 = (bf16[2,2,128]{2,1,0:T(2,128)(2,1)S(1)}, bf16[2,2,128]{2,1,0:T(2,128)(2,1)}, u32[]{:S(2)}) copy-start(bf16[2,2,128]{2,1,0:T(2,128)(2,1)} %param.16) | copy-start | bytes 3076
  1046.4 121.3 %copy-start.22 = (bf16[1,128,512]{2,1,0:T(8,128)(2,1)S(1)}, bf16[1,128,512]{2,1,0:T(8,128)(2,1)}, u32[]{:S(2)}) copy-start(bf16[1,128,512]{2,1,0:T(8,128)(2,1)} %get-tuple-element.22) | copy-start | bytes 393220
  1046.4 121.4 %copy-start.3 = (f32[128,512]{1,0:T(8,128)S(1)}, f32[128,512]{1,0:T(8,128)}, u32[]{:S(2)}) copy-start(f32[128,512]{1,0:T(8,128)} %copy-done.2) | copy-start | bytes 786436
  1046.4 121.4 %copy-start.11 = (f32[128,512]{1,0:T(8,128)S(1)}, f32[128,512]{1,0:T(8,128)}, u32[]{:S(2)}) copy-start(f32[128,512]{1,0:T(8,128)} %copy-done.10) | copy-start | bytes 786436
  1046.4 121.4 %copy-start.27 = (f32[128]{0:T(128)S(1)}, f32[128]{0:T(128)}, u32[]{:S(2)}) copy-start(f32[128]{0:T(128)} %copy-done.26) | copy-start | bytes 1540
  1046.4 121.4 %copy-start.30 = (f32[128]{0:T(128)S(1)}, f32[128]{0:T(128)}, u32[]{:S(2)}) copy-start(f32[128]{0:T(128)} %copy-done.29) | copy-start | bytes 1540
  1046.5 121.4 %copy-start.35 = (bf16[2,128,128]{2,1,0:T(8,128)(2,1)S(1)}, bf16[2,128,128]{2,1,0:T(8,128)(2,1)}, u32[]{:S(2)}) copy-start(bf16[2,128,128]{2,1,0:T(8,128)(2,1)} %param.15) | copy-start | bytes 196612
  1159.4 190.3 %all-to-all-start.5 = ((bf16[32,512,512]{2,0,1:T(8,128)(2,1)}), bf16[32,512,512]{2,0,1:T(8,128)(2,1)}, u32[]{:S(2)}, u32[]{:S(2)}) async-start(bf16[32,512,512]{2,0,1:T(8,128)(2,1)} %copy.189), calls=%async_computation.5 | async-start | bytes 33554432 | tf_op jit(solution)/shard_map/all_to_all | solution.py:37
  1167.9 278.0 %copy-start.20 = (bf16[1,128,512]{1,2,0:T(8,128)(2,1)}, bf16[1,128,512]{1,2,0:T(8,128)(2,1)S(1)}, u32[]{:S(2)}) copy-start(bf16[1,128,512]{1,2,0:T(8,128)(2,1)S(1)} %copy.245) | copy-start | bytes 393220
  1408.6 37.3 %copy-start.38 = (f32[128]{0:T(128)S(1)}, f32[128]{0:T(128)}, u32[]{:S(2)}) copy-start(f32[128]{0:T(128)} %get-tuple-element.28) | copy-start | bytes 1540
  1408.6 37.3 %copy-start.41 = (f32[128]{0:T(128)S(1)}, f32[128]{0:T(128)}, u32[]{:S(2)}) copy-start(f32[128]{0:T(128)} %get-tuple-element.31) | copy-start | bytes 1540
  1438.2 58.6 %copy-start.4 = (f32[128,512]{1,0:T(8,128)}, f32[128,512]{1,0:T(8,128)S(1)}, u32[]{:S(2)}) copy-start(f32[128,512]{1,0:T(8,128)S(1)} %broadcast_multiply_fusion.5) | copy-start | bytes 786436
  1445.9 50.9 %copy-start.16 = (f32[128,512]{1,0:T(8,128)}, f32[128,512]{1,0:T(8,128)S(1)}, u32[]{:S(2)}) copy-start(f32[128,512]{1,0:T(8,128)S(1)} %add_rsqrt_fusion.5) | copy-start | bytes 786436
  1445.9 50.9 %copy-start.15 = (f32[128,512]{1,0:T(8,128)S(1)}, f32[128,512]{1,0:T(8,128)}, u32[]{:S(2)}) copy-start(f32[128,512]{1,0:T(8,128)} %copy-done.14) | copy-start | bytes 786436
  1630.5 372.5 %all-to-all-start.2 = ((bf16[2,128,128,512]{3,0,2,1:T(2,128)(2,1)}), bf16[2,128,128,512]{3,0,2,1:T(2,128)(2,1)}, u32[]{:S(2)}, u32[]{:S(2)}) async-start(bf16[2,128,128,512]{3,0,2,1:T(2,128)(2,1)} %copy.169), calls=%async_computation.2 | async-start | bytes 67108864 | tf_op jit(solution)/shard_map/all_to_all | solution.py:35
  1640.6 31.9 %copy-start.33 = (bf16[2,128,128]{2,1,0:T(8,128)(2,1)S(1)}, bf16[2,128,128]{2,1,0:T(8,128)(2,1)}, u32[]{:S(2)}) copy-start(bf16[2,128,128]{2,1,0:T(8,128)(2,1)} %param.17) | copy-start | bytes 196612
  1672.6 37.4 %copy-start.21 = (bf16[1,128,512]{1,2,0:T(8,128)(2,1)S(1)}, bf16[1,128,512]{1,2,0:T(8,128)(2,1)}, u32[]{:S(2)}) copy-start(bf16[1,128,512]{1,2,0:T(8,128)(2,1)} %copy-done.20) | copy-start | bytes 393220
  1672.6 37.4 %copy-start.39 = (f32[128]{0:T(128)S(1)}, f32[128]{0:T(128)}, u32[]{:S(2)}) copy-start(f32[128]{0:T(128)} %get-tuple-element.28) | copy-start | bytes 1540
  1672.6 37.4 %copy-start.42 = (f32[128]{0:T(128)S(1)}, f32[128]{0:T(128)}, u32[]{:S(2)}) copy-start(f32[128]{0:T(128)} %get-tuple-element.31) | copy-start | bytes 1540
  1702.2 58.6 %copy-start.8 = (f32[128,512]{1,0:T(8,128)}, f32[128,512]{1,0:T(8,128)S(1)}, u32[]{:S(2)}) copy-start(f32[128,512]{1,0:T(8,128)S(1)} %broadcast_multiply_fusion.1) | copy-start | bytes 786436
  1710.0 50.9 %copy-start.18 = (f32[128,512]{1,0:T(8,128)}, f32[128,512]{1,0:T(8,128)S(1)}, u32[]{:S(2)}) copy-start(f32[128,512]{1,0:T(8,128)S(1)} %add_rsqrt_fusion.1) | copy-start | bytes 786436
  1710.0 50.9 %copy-start.13 = (f32[128,512]{1,0:T(8,128)S(1)}, f32[128,512]{1,0:T(8,128)}, u32[]{:S(2)}) copy-start(f32[128,512]{1,0:T(8,128)} %copy-done.12) | copy-start | bytes 786436
  2003.0 372.4 %all-to-all-start.6 = ((bf16[2,128,128,512]{3,0,2,1:T(2,128)(2,1)}), bf16[2,128,128,512]{3,0,2,1:T(2,128)(2,1)}, u32[]{:S(2)}, u32[]{:S(2)}) async-start(bf16[2,128,128,512]{3,0,2,1:T(2,128)(2,1)} %copy.196), calls=%async_computation.6 | async-start | bytes 67108864 | tf_op jit(solution)/shard_map/all_to_all | solution.py:35
  2375.4 190.0 %all-to-all-start.3 = ((bf16[32,512,512]{2,0,1:T(8,128)(2,1)}), bf16[32,512,512]{2,0,1:T(8,128)(2,1)}, u32[]{:S(2)}, u32[]{:S(2)}) async-start(bf16[32,512,512]{2,0,1:T(8,128)(2,1)} %copy.173), calls=%async_computation.3 | async-start | bytes 33554432 | tf_op jit(solution)/shard_map/all_to_all | solution.py:37
  2515.5 57.5 %copy-start.47 = (f32[128]{0:T(128)S(1)}, f32[128]{0:T(128)}, u32[]{:S(2)}) copy-start(f32[128]{0:T(128)} %get-tuple-element.10) | copy-start | bytes 1540
  2515.5 57.7 %copy-start.46 = (f32[128]{0:T(128)S(1)}, f32[128]{0:T(128)}, u32[]{:S(2)}) copy-start(f32[128]{0:T(128)} %get-tuple-element.13) | copy-start | bytes 1540
  2565.4 190.2 %all-to-all-start.7 = ((bf16[32,512,512]{2,0,1:T(8,128)(2,1)}), bf16[32,512,512]{2,0,1:T(8,128)(2,1)}, u32[]{:S(2)}, u32[]{:S(2)}) async-start(bf16[32,512,512]{2,0,1:T(8,128)(2,1)} %copy.200), calls=%async_computation.7 | async-start | bytes 33554432 | tf_op jit(solution)/shard_map/all_to_all | solution.py:37
  2820.0 25.2 copy-start.9
  2820.0 25.2 copy-start.19
  2820.0 25.2 copy-start.37
  2820.1 25.1 copy-start.40
  2820.1 25.1 copy-start.43
  2912.2 25.2 copy-start.5
  2912.2 25.2 copy-start.17
  (8 other events, 100.9 us)
where the time goes:
time: 3010 us; the launch traced here: 2990 us
  waiting for transfers between devices  1170 us (39%)
  local copies, waits for them, and re-layouts  887 us (29%)
  matrix products  497 us (17%)
  other arithmetic  363 us (12%)
  starting transfers between devices  69.2 us (2%)
    all_to_all x4, waiting for transfers between devices, tri_update(): sides_chan = lax.all_to_all(sides, 'dap', 1, 2, tiled=True)  736 us
    all_to_all x4, waiting for transfers between devices, tri_update(): t_rows = lax.all_to_all(tri_prod, 'dap', 1, 0, tiled=True)  438 us
    convert_element_type x4, local copies, waits for them, and re-layouts, project_rows(): (keep_mask * jax.nn.sigmoid(projected[:, 1]) * projected[:, 0]).astype(jn...  323 us
    convert_element_type x4, other arithmetic, project_rows(): (keep_mask * jax.nn.sigmoid(projected[:, 1]) * projected[:, 0]).astype(jn...  211 us
    dot_general x4, matrix products, project_rows(): jnp.einsum('rnz,zsgc->sgcrn', x_norm, w_split, preferred_element_type=jnp...  203 us
    slice x8, local copies, waits for them, and re-layouts, tri_update(): sides_chan[1]  112 us
    dot_general x4, matrix products, finish_rows(): jnp.einsum('crn,cz->rnz', t_norm, w_out, preferred_element_type=jnp.float32)  109 us
    dot_general x4, matrix products, finish_rows(): jnp.einsum('rnz,zy->rny', x_norm, w_gate, preferred_element_type=jnp.floa...  97.3 us
  transfers between devices with their start and end apart: 8, of which 8 were waited for; matrix products, arithmetic and copies ran while one was open for 34% of the time, Pallas kernels for 0%

commit v1 on v0

v1 whole, which is shorter than its diff:
```python
import functools

import jax
import jax.numpy as jnp
from jax import lax
from jax.experimental import pallas as pl
from jax.experimental.pallas import tpu as pltpu
from jax.sharding import PartitionSpec as P


F32, BF16 = jnp.float32, jnp.bfloat16
ROWS, N, C = 128, 512, 128
RB = 16
UNROLL = 8
CG = 8
CHUNK = 32
ACROSS = [(0, 2), (2, 0), (1, 3), (3, 1)]
ON_CHIP = [(0, 1), (1, 0), (2, 3), (3, 2)]


def cost(us):
    return pl.CostEstimate(flops=int(us * 4e8), bytes_accessed=int(us * 2e6), transcendentals=0)


def ln_rows(v, gain, shift):
    cen = v - jnp.mean(v, axis=-1, keepdims=True)
    var = jnp.mean(cen * cen, axis=-1, keepdims=True)
    return (cen * lax.rsqrt(var + 1e-5) * gain + shift).astype(BF16)


def sigmoid(v):
    return 0.5 * jnp.tanh(0.5 * v) + 0.5


def dot_nt(a, b):
    return lax.dot_general(a, b, (((1,), (1,)), ((), ())), preferred_element_type=F32)


def dot_tn(a, b):
    return lax.dot_general(a, b, (((0,), (0,)), ((), ())), preferred_element_type=F32)


def cat(refs, c, axis=0):
    return refs[0][c] if len(refs) == 1 else jnp.concatenate([r[c] for r in refs], axis=axis)


def proj_body(z_ref, m_ref, n_ref, w_ref, scr):
    gain, shift = n_ref[0:1, :], n_ref[1:2, :]

    def row(i, carry):
        x = ln_rows(z_ref[i].astype(F32), gain, shift)
        keep = m_ref[i].astype(F32)
        for side in range(2):
            pg = dot_nt(w_ref[side * 256:(side + 1) * 256, :], x)
            scr[side, i] = (keep * sigmoid(pg[128:]) * pg[:128]).astype(BF16)
        return carry

    lax.fori_loop(0, RB, row, 0, unroll=UNROLL)


def proj_out_kernel(z_ref, m_ref, n_ref, w_ref, a_ref, b_ref, scr):
    proj_body(z_ref, m_ref, n_ref, w_ref, scr)
    a_ref[...] = jnp.transpose(scr[0], (1, 0, 2))
    b_ref[...] = jnp.transpose(scr[1], (1, 0, 2))


def proj_in_kernel(pos_ref, z_ref, m_ref, n_ref, w_ref, mine_ref, other_ref, b_ref, scr):
    proj_body(z_ref, m_ref, n_ref, w_ref, scr)
    for k in range(2):
        mine, other = (pl.multiple_of(pos_ref[2 * o + k] * ROWS, ROWS) for o in range(2))
        lanes = pl.ds(k * ROWS, ROWS)
        mine_ref[:, :, lanes] = jnp.transpose(scr[0, :, :, pl.ds(mine, ROWS)], (1, 0, 2))
        other_ref[:, :, lanes] = jnp.transpose(scr[0, :, :, pl.ds(other, ROWS)], (1, 0, 2))
    b_ref[...] = jnp.transpose(scr[1], (1, 0, 2))


def whole(shape):
    return pl.BlockSpec(shape, lambda r, *_: (0,) * len(shape))


def project(z, mask, norm, w_t, pos=None):
    rows = z.shape[0]
    slab = lambda lanes: pl.BlockSpec((C, RB, lanes), lambda r, *_: (0, r, 0))
    lanes = (N, N) if pos is None else (2 * ROWS, 2 * ROWS, N)
    grid_spec = pltpu.PrefetchScalarGridSpec(
        num_scalar_prefetch=0 if pos is None else 1, grid=(rows // RB,),
        in_specs=[pl.BlockSpec((RB, N, C), lambda r, *_: (r, 0, 0)), pl.BlockSpec((RB, 1, N), lambda r, *_: (r, 0, 0)),
                  whole((2, C)), whole((4 * C, C))],
        out_specs=[slab(w) for w in lanes],
        scratch_shapes=[pltpu.VMEM((2, RB, C, N), BF16)])
    args = (z, mask.reshape(rows, 1, N), norm, w_t)
    return pl.pallas_call(
        proj_out_kernel if pos is None else proj_in_kernel, grid_spec=grid_spec,
        out_shape=[jax.ShapeDtypeStruct((C, rows, w), BF16) for w in lanes],
        cost_estimate=cost(0.4 * rows))(*(args if pos is None else (pos,) + args))


def finish_kernel(t_ref, z_ref, n_ref, mid_ref, wg_ref, wo_ref, o_ref, scr):
    gain, shift = n_ref[0:1, :], n_ref[1:2, :]
    mid_gain, mid_shift = mid_ref[0], mid_ref[1]
    scr[...] = jnp.transpose(t_ref[...], (1, 0, 2))

    def row(i, carry):
        v = scr[i].astype(F32)
        cen = v - jnp.mean(v, axis=0, keepdims=True)
        var = jnp.mean(cen * cen, axis=0, keepdims=True)
        y = (cen * lax.rsqrt(var + 1e-5) * mid_gain + mid_shift).astype(BF16)
        update = dot_tn(y, wo_ref[...])
        z_row = z_ref[i].astype(F32)
        gate = sigmoid(jnp.dot(ln_rows(z_row, gain, shift), wg_ref[...], preferred_element_type=F32))
        o_ref[i] = (z_row + gate * update).astype(BF16)
        return carry

    lax.fori_loop(0, RB, row, 0, unroll=UNROLL)


def finish(t, z, norm, mid, w_gate, w_out, first=0, rows=ROWS):
    start = first // RB
    return pl.pallas_call(
        finish_kernel, grid=(rows // RB,), out_shape=jax.ShapeDtypeStruct((rows, N, C), BF16),
        in_specs=[pl.BlockSpec((C, RB, N), lambda r: (0, r + start, 0)), pl.BlockSpec((RB, N, C), lambda r: (r + start, 0, 0)),
                  whole((2, C)), whole((2, C, 1)), whole((C, C)), whole((C, C))],
        out_specs=pl.BlockSpec((RB, N, C), lambda r: (r, 0, 0)),
        scratch_shapes=[pltpu.VMEM((RB, C, N), BF16)], cost_estimate=cost(0.44 * rows))(t, z, norm, mid, w_gate, w_out)


def contract_out_kernel(counts, pos_ref, *refs):
    na, nb, nr = counts
    a_refs, b_refs, r_refs, (t0_ref, t1_ref) = refs[:na], refs[na:na + nb], refs[na + nb:na + nb + nr], refs[na + nb + nr:]
    for c in range(CG):
        a = cat(a_refs, c)
        for o, side in enumerate((b_refs, r_refs)):
            t = dot_nt(a, cat(side, c)).astype(BF16)
            for k in range(2):
                lanes = pl.ds(pl.multiple_of(pos_ref[2 * o + k] * ROWS, ROWS), ROWS)
                t0_ref[c, :, lanes] = t[:ROWS, k * ROWS:(k + 1) * ROWS]
                t1_ref[c, :, lanes] = t[ROWS:, k * ROWS:(k + 1) * ROWS]


def contract_out(pos, a, b, r):
    part = lambda v: pl.BlockSpec((CG,) + v.shape[1:], lambda g, *_: (g, 0, 0))
    ops = list(a) + list(b) + list(r)
    t = jax.ShapeDtypeStruct((C, ROWS, N), BF16)
    grid_spec = pltpu.PrefetchScalarGridSpec(num_scalar_prefetch=1, grid=(C // CG,), in_specs=[part(v) for v in ops],
                                             out_specs=[part(t)] * 2)
    return pl.pallas_call(functools.partial(contract_out_kernel, (len(a), len(b), len(r))), grid_spec=grid_spec,
                          out_shape=[t, t], cost_estimate=cost(50))(pos, *ops)


def contract_in_kernel(count, *refs):
    a_refs, b_refs, t_ref = refs[:count], refs[count:2 * count], refs[2 * count]
    for c in range(CG):
        t_ref[c] = dot_tn(cat(a_refs, c), cat(b_refs, c)).astype(BF16)


def contract_in(a, b, slot):
    t = jax.ShapeDtypeStruct((C, ROWS, N), BF16)
    return pl.pallas_call(
        functools.partial(contract_in_kernel, len(a)), grid=(C // CG,), out_shape=t,
        in_specs=[pl.BlockSpec((CG, v.shape[1], ROWS), lambda g: (g, 0, slot)) for v in a]
        + [pl.BlockSpec((CG, v.shape[1], N), lambda g: (g, 0, 0)) for v in b],
        out_specs=pl.BlockSpec((CG, ROWS, N), lambda g: (g, 0, 0)), cost_estimate=cost(30))(*a, *b)


def solution(mesh):
    row_spec, mask_spec, replicated = P(("data", "dap"), None, None), P(("data", "dap"), None), P()

    def across(v):
        return lax.ppermute(v, "dap", ACROSS)

    def on_chip(v):
        return lax.ppermute(v, "dap", ON_CHIP)

    def update_crops(z_one, mask_one, z_two, mask_two, norm_in, w_proj, w_gate, norm_mid, w_out):
        me = lax.axis_index("dap")
        chip, core = me // 2, me % 2
        first = chip == 0
        pos = jnp.stack([2 * chip + core, 2 * (1 - chip) + core, 2 * chip + 1 - core, 2 * (1 - chip) + 1 - core]).astype(jnp.int32)
        norm_in, norm_mid = norm_in.astype(F32), norm_mid.astype(F32)[..., None]
        w_t = jnp.swapaxes(w_proj, 1, 2)

        pieces = [slice(r, r + CHUNK) for r in range(0, ROWS, CHUNK)]
        mask_got = across(jnp.where(first, mask_two, mask_one))
        z_got = []
        for p in pieces:
            z_got.append(across(jnp.where(first, z_two[p], z_one[p])))
        z_own = jnp.where(first, z_one, z_two)
        mask_own = jnp.where(first, mask_one, mask_two)

        a_own, b_own = project(z_own, mask_own, norm_in[0], w_t[0])
        a, b = map(list, zip((a_own, b_own), *(project(z, mask_got[p], norm_in[0], w_t[0]) for z, p in zip(z_got, pieces))))
        t = contract_out(pos, a, b, [on_chip(v) for v in b])
        z_got = jnp.concatenate(z_got, axis=0)
        z_mid = [finish(t[s], z, norm_in[0], norm_mid[0], w_gate[0], w_out[0]) for s, z in enumerate((z_own, z_got))]

        mine, other, b = map(list, zip(*(project(z_mid[s], m, norm_in[1], w_t[1], pos) for s, m in enumerate((mask_own, mask_got)))))
        a = mine + [on_chip(v) for v in other]
        b = b + [on_chip(v) for v in b]
        t_back = contract_in(a, b, 1)
        back = [across(finish(t_back, z_mid[1], norm_in[1], norm_mid[1], w_gate[1], w_out[1], p.start, CHUNK)) for p in pieces]
        own = finish(contract_in(a, b, 0), z_mid[0], norm_in[1], norm_mid[1], w_gate[1], w_out[1])
        back = jnp.concatenate(back, axis=0)
        return jnp.where(first, own, back), jnp.where(first, back, own)

    return jax.shard_map(update_crops, mesh=mesh,
                         in_specs=(row_spec, mask_spec, row_spec, mask_spec) + (replicated,) * 5,
                         out_specs=(row_spec, row_spec), check_vma=False)
```

time: 3010 us -> 1250 us (0.42)
  local copies, waits for them, and re-layouts: 887 us -> 20.6 us
  waiting for transfers between devices: 1170 us -> 596 us
  Pallas kernels: 0 us -> 546 us
  matrix products: 497 us -> 0 us
  other arithmetic: 363 us -> 64.6 us
  starting transfers between devices: 69.2 us -> 12.7 us
    all_to_all x8 -> x0, waiting for transfers between devices: 1170 us -> none  [the longest x4 736 us: tri_update(): sides_chan = lax.all_to_all(sides, 'dap', 1, 2, tiled=True)]
    ppermute x0 -> x18, waiting for transfers between devices: none -> 596 us  [the longest x9 548 us: across(): return lax.ppermute(v, 'dap', ACROSS)]
    pallas_call x0 -> x17, Pallas kernels: none -> 546 us  [the longest x7 226 us: finish(): pl.pallas_call(finish_kernel, grid=(rows // RB,), out_shape=jax.ShapeDtyp...]
    dot_general x16 -> x0, matrix products: 497 us -> none  [the longest x4 203 us: project_rows(): jnp.einsum('rnz,zsgc->sgcrn', x_norm, w_split, preferred_element_type=jnp...]
    convert_element_type x18 -> x0, local copies, waits for them, and re-layouts: 454 us -> none  [the longest x4 323 us: project_rows(): (keep_mask * jax.nn.sigmoid(projected[:, 1]) * projected[:, 0]).astype(jn...]
    convert_element_type x9 -> x2, other arithmetic: 273 us -> 0.68 us  [update_crops(): norm_in, norm_mid = (norm_in.astype(F32), norm_mid.astype(F32)[..., None])]
    slice x13 -> x0, local copies, waits for them, and re-layouts: 177 us -> none  [the longest x8 112 us: tri_update(): sides_chan[1]]
    all_to_all x6 -> x0, local copies, waits for them, and re-layouts: 116 us -> none  [the longest x4 91.5 us: tri_update(): sides_chan = lax.all_to_all(sides, 'dap', 1, 2, tiled=True)]
  transfers between devices with their start and end apart: 8 -> 18, of which waited for: 8 -> 6; matrix products, arithmetic and copies ran while one was open for 34% -> 4% of each run, Pallas kernels for 0% -> 23%
where the time goes in v1:
time: 1250 us; the launch traced here: 1240 us
  waiting for transfers between devices  596 us (48%)
  Pallas kernels  546 us (44%)
  other arithmetic  64.6 us (5%)
  local copies, waits for them, and re-layouts  20.6 us (2%)
  starting transfers between devices  12.7 us (1%)
    ppermute x9, waiting for transfers between devices, across(): return lax.ppermute(v, 'dap', ACROSS)  548 us
    pallas_call x7, Pallas kernels, finish(): pl.pallas_call(finish_kernel, grid=(rows // RB,), out_shape=jax.ShapeDtyp...  226 us
    pallas_call x7, Pallas kernels, project(): pl.pallas_call(proj_out_kernel if pos is None else proj_in_kernel, grid_s...  203 us
    pallas_call x2, Pallas kernels, contract_in(): pl.pallas_call(functools.partial(contract_in_kernel, len(a)), grid=(C //...  69.7 us
    ppermute x9, waiting for transfers between devices, on_chip(): return lax.ppermute(v, 'dap', ON_CHIP)  48.2 us
    pallas_call x1, Pallas kernels, contract_out(): pl.pallas_call(functools.partial(contract_out_kernel, (len(a), len(b), le...  47.6 us
  transfers between devices with their start and end apart: 18, of which 6 were waited for; matrix products, arithmetic and copies ran while one was open for 4% of the time, Pallas kernels for 23%

profile of v1, /device:TPU:0, one launch (start us, length us, event | category | flops | bytes accessed | tf_op | source)
XLA Modules:
  0.0 1241.5 jit_solution(16918788933392967586)
XLA Ops:
  0.6 1.1 broadcast_select_fusion.3
  1.7 1.0 copy.33.m_ref
  4.0 1.1 copy.32
  5.1 0.7 slice_bitcast_fusion
  5.8 14.1 %broadcast_select_fusion.2.z_ref = bf16[128,512,128]{2,1,0:T(8,128)(2,1)} fusion(bf16[128,512,128]{2,1,0:T(8,128)(2,1)} %param.9, bf16[128,512,128]{2,1,0:T(8,128)(2,1)} %param.11, pred[]{:T(512)S(6)} %eq.5), kind=kLoop, calls=%fused_computation.3 | loop fusion | flops 8388608 | bytes 50331648 | tf_op jit(solution)/shard_map/jit(_where)/select_n | solution.py:187
  19.9 47.3 %shard_map.104 = (bf16[128,128,512]{2,1,0:T(8,128)(2,1)}, bf16[128,128,512]{2,1,0:T(8,128)(2,1)}) custom-call(bf16[128,512,128]{2,1,0:T(8,128)(2,1)} %broadcast_select_fusion.2.z_ref, s32[128,1,512]{2,1,0:T(1,128)} %copy.33.m_ref, f32[2,128]{1,0:T(2,128)} %get-tuple-element.59.n_ref, bf16[512,128]{1,0:T(8,128)(2,1)} %get-tuple-element.47.w_ref), custom_call_target="tpu_custom_call" | custom-call | flops 20480000000 | bytes 102400000 | tf_op jit(solution)/shard_map/pallas_call | solution.py:92
  67.2 0.8 collective-permute-start.5
  68.0 15.9 %slice_select_fusion = (bf16[32,512,128]{2,1,0:T(8,128)(2,1)}, bf16[32,512,128]{2,1,0:T(8,128)(2,1)}, bf16[32,512,128]{2,1,0:T(8,128)(2,1)S(1)}, bf16[32,512,128]{2,1,0:T(8,128)(2,1)}) fusion(bf16[128,512,128]{2,1,0:T(8,128)(2,1)} %param.9, bf16[128,512,128]{2,1,0:T(8,128)(2,1)} %param.11, pred[]{:T(512)S(6)} %eq.5), kind=kLoop, calls=%fused_computation.4 | loop fusion | flops 8388608 | bytes 50331648 | tf_op jit(solution)/shard_map/jit(_where)/select_n | solution.py:186
  84.0 2.5 collective-permute-start
  86.5 2.0 collective-permute-start.3
  88.5 274.6 %collective-permute-done.1 = s32[128,512]{1,0:T(8,128)S(1)} collective-permute-done((s32[128,512]{1,0:T(8,128)S(1)}, s32[128,512]{1,0:T(8,128)S(1)}, u32[]{:S(2)}, u32[]{:S(2)}) %collective-permute-start.1) | collective-permute-done | bytes 262176 | tf_op jit(solution)/shard_map/ppermute | solution.py:169
  363.1 1.7 collective-permute-start.4
  364.8 0.7 copy.34.m_ref
  365.5 0.7 copy.35.m_ref
  366.2 0.7 copy.36.m_ref
  366.9 0.7 copy.37.m_ref
  367.6 14.4 %shard_map.105 = (bf16[128,32,512]{2,1,0:T(8,128)(2,1)}, bf16[128,32,512]{2,1,0:T(8,128)(2,1)}) custom-call(bf16[32,512,128]{2,1,0:T(8,128)(2,1)} %collective-permute-done.z_ref, s32[32,1,512]{2,1,0:T(1,128)} %copy.34.m_ref, f32[2,128]{1,0:T(2,128)} %get-tuple-element.59.n_ref, bf16[512,128]{1,0:T(8,128)(2,1)} %get-tuple-element.47.w_ref), custom_call_target="tpu_custom_call" | custom-call | flops 5120000000 | bytes 25600000 | tf_op jit(solution)/shard_map/pallas_call | solution.py:92
  382.0 14.4 %shard_map.106 = (bf16[128,32,512]{2,1,0:T(8,128)(2,1)}, bf16[128,32,512]{2,1,0:T(8,128)(2,1)}) custom-call(bf16[32,512,128]{2,1,0:T(8,128)(2,1)} %collective-permute-done.2.z_ref, s32[32,1,512]{2,1,0:T(1,128)} %copy.35.m_ref, f32[2,128]{1,0:T(2,128)} %get-tuple-element.59.n_ref, bf16[512,128]{1,0:T(8,128)(2,1)} %get-tuple-element.47.w_ref), custom_call_target="tpu_custom_call" | custom-call | flops 5120000000 | bytes 25600000 | tf_op jit(solution)/shard_map/pallas_call | solution.py:92
  396.9 14.5 %shard_map.107 = (bf16[128,32,512]{2,1,0:T(8,128)(2,1)}, bf16[128,32,512]{2,1,0:T(8,128)(2,1)}) custom-call(bf16[32,512,128]{2,1,0:T(8,128)(2,1)} %collective-permute-done.3.z_ref, s32[32,1,512]{2,1,0:T(1,128)} %copy.36.m_ref, f32[2,128]{1,0:T(2,128)} %get-tuple-element.59.n_ref, bf16[512,128]{1,0:T(8,128)(2,1)} %get-tuple-element.47.w_ref), custom_call_target="tpu_custom_call" | custom-call | flops 5120000000 | bytes 25600000 | tf_op jit(solution)/shard_map/pallas_call | solution.py:92
  411.6 44.2 %collective-permute-done.4.z_ref = bf16[32,512,128]{2,1,0:T(8,128)(2,1)} collective-permute-done((bf16[32,512,128]{2,1,0:T(8,128)(2,1)}, bf16[32,512,128]{2,1,0:T(8,128)(2,1)}, u32[]{:S(2)}, u32[]{:S(2)}) %collective-permute-start.4) | collective-permute-done | bytes 4194336 | tf_op jit(solution)/shard_map/ppermute | solution.py:169
  455.8 14.4 %shard_map.108 = (bf16[128,32,512]{2,1,0:T(8,128)(2,1)}, bf16[128,32,512]{2,1,0:T(8,128)(2,1)}) custom-call(bf16[32,512,128]{2,1,0:T(8,128)(2,1)} %collective-permute-done.4.z_ref, s32[32,1,512]{2,1,0:T(1,128)} %copy.37.m_ref, f32[2,128]{1,0:T(2,128)} %get-tuple-element.59.n_ref, bf16[512,128]{1,0:T(8,128)(2,1)} %get-tuple-element.47.w_ref), custom_call_target="tpu_custom_call" | custom-call | flops 5120000000 | bytes 25600000 | tf_op jit(solution)/shard_map/pallas_call | solution.py:92
  470.3 0.8 copy.38.mid_ref
  472.3 0.9 reshape.32.m_ref
  473.2 13.9 %pad_maximum_fusion.z_ref = bf16[128,512,128]{2,1,0:T(8,128)(2,1)} fusion(bf16[32,512,128]{2,1,0:T(8,128)(2,1)} %collective-permute-done.4.z_ref, bf16[32,512,128]{2,1,0:T(8,128)(2,1)} %collective-permute-done.3.z_ref, bf16[32,512,128]{2,1,0:T(8,128)(2,1)} %collective-permute-done.2.z_ref, bf16[32,512,128]{2,1,0:T(8,128)(2,1)} %collective-permute-done.z_ref), kind=kLoop, calls=%fused_computation | loop fusion | flops 25165824 | bytes 33554432 | tf_op jit(solution)/shard_map/concatenate | solution.py:193
  487.2 47.6 %shard_map.109 = (bf16[128,128,512]{2,1,0:T(8,128)(2,1)}, bf16[128,128,512]{2,1,0:T(8,128)(2,1)}) custom-call(s32[4]{0:T(128)} %pad_add_fusion.pos_ref, bf16[128,128,512]{2,1,0:T(8,128)(2,1)} %get-tuple-element.20.refs_0_, bf16[128,32,512]{2,1,0:T(8,128)(2,1)} %get-tuple-element.21.refs_1_, bf16[128,32,512]{2,1,0:T(8,128)(2,1)} %get-tuple-element.22.refs_2_, ...), custom_call_target="tpu_custom_call" | custom-call | flops 20000000000 | bytes 100000000 | tf_op jit(solution)/shard_map/pallas_call | solution.py:146
  534.8 53.7 %shard_map.112.z_ref = bf16[128,512,128]{2,1,0:T(8,128)(2,1)} custom-call(bf16[128,128,512]{2,1,0:T(8,128)(2,1)} %get-tuple-element.32.t_ref, bf16[128,512,128]{2,1,0:T(8,128)(2,1)} %pad_maximum_fusion.z_ref, f32[2,128]{1,0:T(2,128)} %get-tuple-element.59.n_ref, f32[2,128,1]{2,1,0:T(8,128)} %copy.38.mid_ref, bf16[128,128]{1,0:T(8,128)(2,1)} %get-tuple-element.60.wg_ref, ...), custom_call_target="tpu_custom_call" | custom-call | flops 22528000000 | bytes 112640000 | tf_op jit(solution)/shard_map/pallas_call | solution.py:119
  588.5 49.1 %shard_map.113 = (bf16[128,128,256]{2,1,0:T(8,128)(2,1)}, bf16[128,128,256]{2,1,0:T(8,128)(2,1)}, bf16[128,128,512]{2,1,0:T(8,128)(2,1)}) custom-call(s32[4]{0:T(128)} %pad_add_fusion.pos_ref, bf16[128,512,128]{2,1,0:T(8,128)(2,1)} %shard_map.112.z_ref, s32[128,1,512]{2,1,0:T(1,128)} %reshape.32.m_ref, f32[2,128]{1,0:T(2,128)} %get-tuple-element.58.n_ref, ...), custom_call_target="tpu_custom_call" | custom-call | flops 20480000000 | bytes 102400000 | tf_op jit(solution)/shard_map/pallas_call | solution.py:92
  638.1 53.7 %shard_map.110.z_ref = bf16[128,512,128]{2,1,0:T(8,128)(2,1)} custom-call(bf16[128,128,512]{2,1,0:T(8,128)(2,1)} %get-tuple-element.30.t_ref, bf16[128,512,128]{2,1,0:T(8,128)(2,1)} %broadcast_select_fusion.2.z_ref, f32[2,128]{1,0:T(2,128)} %get-tuple-element.59.n_ref, f32[2,128,1]{2,1,0:T(8,128)} %copy.38.mid_ref, ...), custom_call_target="tpu_custom_call" | custom-call | flops 22528000000 | bytes 112640000 | tf_op jit(solution)/shard_map/pallas_call | solution.py:119
  691.8 48.8 %shard_map.111 = (bf16[128,128,256]{2,1,0:T(8,128)(2,1)}, bf16[128,128,256]{2,1,0:T(8,128)(2,1)}, bf16[128,128,512]{2,1,0:T(8,128)(2,1)}) custom-call(s32[4]{0:T(128)} %pad_add_fusion.pos_ref, bf16[128,512,128]{2,1,0:T(8,128)(2,1)} %shard_map.110.z_ref, s32[128,1,512]{2,1,0:T(1,128)} %copy.33.m_ref, f32[2,128]{1,0:T(2,128)} %get-tuple-element.58.n_ref, ...), custom_call_target="tpu_custom_call" | custom-call | flops 20480000000 | bytes 102400000 | tf_op jit(solution)/shard_map/pallas_call | solution.py:92
  741.1 0.8 copy.41.mid_ref
  741.9 36.2 %collective-permute-done.11.refs_3_ = bf16[128,128,256]{2,1,0:T(8,128)(2,1)} collective-permute-done((bf16[128,128,256]{2,1,0:T(8,128)(2,1)}, bf16[128,128,256]{2,1,0:T(8,128)(2,1)}, u32[]{:S(2)}, u32[]{:S(2)}) %collective-permute-start.11) | collective-permute-done | bytes 8388640 | tf_op jit(solution)/shard_map/ppermute | solution.py:172
  778.1 12.0 collective-permute-done.10.refs_2_
  790.1 34.8 %shard_map.116.t_ref = bf16[128,128,512]{2,1,0:T(8,128)(2,1)} custom-call(bf16[128,128,256]{2,1,0:T(8,128)(2,1)} %get-tuple-element.31.refs_0_, bf16[128,128,256]{2,1,0:T(8,128)(2,1)} %get-tuple-element.33.refs_1_, bf16[128,128,256]{2,1,0:T(8,128)(2,1)} %collective-permute-done.10.refs_2_, bf16[128,128,256]{2,1,0:T(8,128)(2,1)} %collective-permute-done.11.refs_3_, ...), custom_call_target="tpu_custom_call" | custom-call | flops 12000000000 | bytes 60000000 | tf_op jit(solution)/shard_map/pallas_call | solution.py:158
  824.9 16.5 %shard_map.119 = bf16[32,512,128]{2,1,0:T(8,128)(2,1)} custom-call(bf16[128,128,512]{2,1,0:T(8,128)(2,1)} %shard_map.116.t_ref, bf16[128,512,128]{2,1,0:T(8,128)(2,1)} %shard_map.112.z_ref, f32[2,128]{1,0:T(2,128)} %get-tuple-element.58.n_ref, f32[2,128,1]{2,1,0:T(8,128)} %copy.41.mid_ref, bf16[128,128]{1,0:T(8,128)(2,1)} %get-tuple-element.61.wg_ref, ...), custom_call_target="tpu_custom_call" | custom-call | flops 5632000000 | bytes 28160000 | tf_op jit(solution)/shard_map/pallas_call | solution.py:119
  841.4 16.1 %shard_map.117 = bf16[32,512,128]{2,1,0:T(8,128)(2,1)} custom-call(bf16[128,128,512]{2,1,0:T(8,128)(2,1)} %shard_map.116.t_ref, bf16[128,512,128]{2,1,0:T(8,128)(2,1)} %shard_map.112.z_ref, f32[2,128]{1,0:T(2,128)} %get-tuple-element.58.n_ref, f32[2,128,1]{2,1,0:T(8,128)} %copy.41.mid_ref, bf16[128,128]{1,0:T(8,128)(2,1)} %get-tuple-element.61.wg_ref, ...), custom_call_target="tpu_custom_call" | custom-call | flops 5632000000 | bytes 28160000 | tf_op jit(solution)/shard_map/pallas_call | solution.py:119
  857.5 1.5 collective-permute-start.14
  859.0 16.1 %shard_map.118 = bf16[32,512,128]{2,1,0:T(8,128)(2,1)} custom-call(bf16[128,128,512]{2,1,0:T(8,128)(2,1)} %shard_map.116.t_ref, bf16[128,512,128]{2,1,0:T(8,128)(2,1)} %shard_map.112.z_ref, f32[2,128]{1,0:T(2,128)} %get-tuple-element.58.n_ref, f32[2,128,1]{2,1,0:T(8,128)} %copy.41.mid_ref, bf16[128,128]{1,0:T(8,128)(2,1)} %get-tuple-element.61.wg_ref, ...), custom_call_target="tpu_custom_call" | custom-call | flops 5632000000 | bytes 28160000 | tf_op jit(solution)/shard_map/pallas_call | solution.py:119
  875.7 1.5 collective-permute-start.15
  877.1 16.2 %shard_map.120 = bf16[32,512,128]{2,1,0:T(8,128)(2,1)} custom-call(bf16[128,128,512]{2,1,0:T(8,128)(2,1)} %shard_map.116.t_ref, bf16[128,512,128]{2,1,0:T(8,128)(2,1)} %shard_map.112.z_ref, f32[2,128]{1,0:T(2,128)} %get-tuple-element.58.n_ref, f32[2,128,1]{2,1,0:T(8,128)} %copy.41.mid_ref, bf16[128,128]{1,0:T(8,128)(2,1)} %get-tuple-element.61.wg_ref, ...), custom_call_target="tpu_custom_call" | custom-call | flops 5632000000 | bytes 28160000 | tf_op jit(solution)/shard_map/pallas_call | solution.py:119
  893.9 34.8 %shard_map.114.t_ref = bf16[128,128,512]{2,1,0:T(8,128)(2,1)} custom-call(bf16[128,128,256]{2,1,0:T(8,128)(2,1)} %get-tuple-element.31.refs_0_, bf16[128,128,256]{2,1,0:T(8,128)(2,1)} %get-tuple-element.33.refs_1_, bf16[128,128,256]{2,1,0:T(8,128)(2,1)} %collective-permute-done.10.refs_2_, bf16[128,128,256]{2,1,0:T(8,128)(2,1)} %collective-permute-done.11.refs_3_, ...), custom_call_target="tpu_custom_call" | custom-call | flops 12000000000 | bytes 60000000 | tf_op jit(solution)/shard_map/pallas_call | solution.py:158
  928.7 53.7 %shard_map.115 = bf16[128,512,128]{2,1,0:T(8,128)(2,1)} custom-call(bf16[128,128,512]{2,1,0:T(8,128)(2,1)} %shard_map.114.t_ref, bf16[128,512,128]{2,1,0:T(8,128)(2,1)} %shard_map.110.z_ref, f32[2,128]{1,0:T(2,128)} %get-tuple-element.58.n_ref, f32[2,128,1]{2,1,0:T(8,128)} %copy.41.mid_ref, bf16[128,128]{1,0:T(8,128)(2,1)} %get-tuple-element.61.wg_ref, ...), custom_call_target="tpu_custom_call" | custom-call | flops 22528000000 | bytes 112640000 | tf_op jit(solution)/shard_map/pallas_call | solution.py:119
  982.5 2.5 constant_dynamic-update-slice_fusion.3
  985.0 146.1 %collective-permute-done.15 = bf16[32,512,128]{2,1,0:T(8,128)(2,1)} collective-permute-done((bf16[32,512,128]{2,1,0:T(8,128)(2,1)}, bf16[32,512,128]{2,1,0:T(8,128)(2,1)}, u32[]{:S(2)}, u32[]{:S(2)}) %collective-permute-start.15) | collective-permute-done | bytes 4194336 | tf_op jit(solution)/shard_map/ppermute | solution.py:169
  1131.0 2.9 constant_dynamic-update-slice_fusion.2
  1134.0 2.9 constant_dynamic-update-slice_fusion.1
  1136.9 83.2 %collective-permute-done.17 = bf16[32,512,128]{2,1,0:T(8,128)(2,1)} collective-permute-done((bf16[32,512,128]{2,1,0:T(8,128)(2,1)}, bf16[32,512,128]{2,1,0:T(8,128)(2,1)}, u32[]{:S(2)}, u32[]{:S(2)}) %collective-permute-start.17) | collective-permute-done | bytes 4194336 | tf_op jit(solution)/shard_map/ppermute | solution.py:169
  1220.1 2.9 constant_dynamic-update-slice_fusion
  1223.0 18.3 %broadcast_select_fusion = (bf16[128,512,128]{2,1,0:T(8,128)(2,1)}, bf16[128,512,128]{2,1,0:T(8,128)(2,1)}) fusion(bf16[128,512,128]{2,1,0:T(8,128)(2,1)S(1)} %constant_dynamic-update-slice_fusion, bf16[128,512,128]{2,1,0:T(8,128)(2,1)} %shard_map.115, pred[]{:T(512)S(6)} %eq.5), kind=kLoop, calls=%fused_computation.1 | loop fusion | flops 16777216 | bytes 67108864 | tf_op jit(solution)/shard_map/jit(_where)/select_n | solution.py:203
  (37 shorter events, 5.4 us)
Async XLA Ops:
  67.2 420.0 %collective-permute-start.5 = (bf16[128,128,512]{2,1,0:T(8,128)(2,1)}, bf16[128,128,512]{2,1,0:T(8,128)(2,1)}, u32[]{:S(2)}, u32[]{:S(2)}) collective-permute-start(bf16[128,128,512]{2,1,0:T(8,128)(2,1)} %get-tuple-element.25.refs_5_), channel_id=1, source_target_pairs={{0,1},{1,0},{2,3},{3,2},{4,5},{5,4},{6,7},{7,6}} | collective-permute-start | bytes 50331656 | tf_op jit(solution)/shard_map/ppermute | solution.py:172
  84.0 283.7 %collective-permute-start = (bf16[32,512,128]{2,1,0:T(8,128)(2,1)S(1)}, bf16[32,512,128]{2,1,0:T(8,128)(2,1)}, u32[]{:S(2)}, u32[]{:S(2)}) collective-permute-start(bf16[32,512,128]{2,1,0:T(8,128)(2,1)S(1)} %get-tuple-element.42), channel_id=1, source_target_pairs={{0,2},{2,0},{1,3},{3,1},{4,6},{6,4},{5,7},{7,5}} | collective-permute-start | bytes 12582920 | tf_op jit(solution)/shard_map/ppermute | solution.py:169
  86.5 295.6 %collective-permute-start.2 = (bf16[32,512,128]{2,1,0:T(8,128)(2,1)}, bf16[32,512,128]{2,1,0:T(8,128)(2,1)}, u32[]{:S(2)}, u32[]{:S(2)}) collective-permute-start(bf16[32,512,128]{2,1,0:T(8,128)(2,1)} %get-tuple-element.41), channel_id=1, source_target_pairs={{0,2},{2,0},{1,3},{3,1},{4,6},{6,4},{5,7},{7,5}} | collective-permute-start | bytes 12582920 | tf_op jit(solution)/shard_map/ppermute | solution.py:169
  86.5 310.5 %collective-permute-start.3 = (bf16[32,512,128]{2,1,0:T(8,128)(2,1)}, bf16[32,512,128]{2,1,0:T(8,128)(2,1)}, u32[]{:S(2)}, u32[]{:S(2)}) collective-permute-start(bf16[32,512,128]{2,1,0:T(8,128)(2,1)} %get-tuple-element.43), channel_id=1, source_target_pairs={{0,2},{2,0},{1,3},{3,1},{4,6},{6,4},{5,7},{7,5}} | collective-permute-start | bytes 12582920 | tf_op jit(solution)/shard_map/ppermute | solution.py:169
  88.5 274.6 %collective-permute-start.1 = (s32[128,512]{1,0:T(8,128)S(1)}, s32[128,512]{1,0:T(8,128)S(1)}, u32[]{:S(2)}, u32[]{:S(2)}) collective-permute-start(s32[128,512]{1,0:T(8,128)S(1)} %get-tuple-element.44), channel_id=1, source_target_pairs={{0,2},{2,0},{1,3},{3,1},{4,6},{6,4},{5,7},{7,5}} | collective-permute-start | bytes 786440 | tf_op jit(solution)/shard_map/ppermute | solution.py:169
  363.1 92.7 %collective-permute-start.4 = (bf16[32,512,128]{2,1,0:T(8,128)(2,1)}, bf16[32,512,128]{2,1,0:T(8,128)(2,1)}, u32[]{:S(2)}, u32[]{:S(2)}) collective-permute-start(bf16[32,512,128]{2,1,0:T(8,128)(2,1)} %get-tuple-element.40), channel_id=1, source_target_pairs={{0,2},{2,0},{1,3},{3,1},{4,6},{6,4},{5,7},{7,5}} | collective-permute-start | bytes 12582920 | tf_op jit(solution)/shard_map/ppermute | solution.py:169
  382.0 105.1 %collective-permute-start.6 = (bf16[128,32,512]{2,1,0:T(8,128)(2,1)}, bf16[128,32,512]{2,1,0:T(8,128)(2,1)}, u32[]{:S(2)}, u32[]{:S(2)}) collective-permute-start(bf16[128,32,512]{2,1,0:T(8,128)(2,1)} %get-tuple-element.26.refs_6_), channel_id=1, source_target_pairs={{0,1},{1,0},{2,3},{3,2},{4,5},{5,4},{6,7},{7,6}} | collective-permute-start | bytes 12582920 | tf_op jit(solution)/shard_map/ppermute | solution.py:172
  396.5 90.7 %collective-permute-start.7 = (bf16[128,32,512]{2,1,0:T(8,128)(2,1)}, bf16[128,32,512]{2,1,0:T(8,128)(2,1)}, u32[]{:S(2)}, u32[]{:S(2)}) collective-permute-start(bf16[128,32,512]{2,1,0:T(8,128)(2,1)} %get-tuple-element.27.refs_7_), channel_id=1, source_target_pairs={{0,1},{1,0},{2,3},{3,2},{4,5},{5,4},{6,7},{7,6}} | collective-permute-start | bytes 12582920 | tf_op jit(solution)/shard_map/ppermute | solution.py:172
  411.5 58.8 %copy-start.2 = (bf16[2,2,128]{2,1,0:T(2,128)(2,1)S(1)}, bf16[2,2,128]{2,1,0:T(2,128)(2,1)}, u32[]{:S(2)}) copy-start(bf16[2,2,128]{2,1,0:T(2,128)(2,1)} %param.16) | copy-start | bytes 3076
  411.5 60.2 %copy-start = (bf16[2,128,128]{2,1,0:T(8,128)(2,1)S(1)}, bf16[2,128,128]{2,1,0:T(8,128)(2,1)}, u32[]{:S(2)}) copy-start(bf16[2,128,128]{2,1,0:T(8,128)(2,1)} %param.17) | copy-start | bytes 196612
  411.5 60.2 %copy-start.1 = (bf16[2,128,128]{2,1,0:T(8,128)(2,1)S(1)}, bf16[2,128,128]{2,1,0:T(8,128)(2,1)}, u32[]{:S(2)}) copy-start(bf16[2,128,128]{2,1,0:T(8,128)(2,1)} %param.15) | copy-start | bytes 196612
  411.5 75.7 %collective-permute-start.8 = (bf16[128,32,512]{2,1,0:T(8,128)(2,1)}, bf16[128,32,512]{2,1,0:T(8,128)(2,1)}, u32[]{:S(2)}, u32[]{:S(2)}) collective-permute-start(bf16[128,32,512]{2,1,0:T(8,128)(2,1)} %get-tuple-element.28.refs_8_), channel_id=1, source_target_pairs={{0,1},{1,0},{2,3},{3,2},{4,5},{5,4},{6,7},{7,6}} | collective-permute-start | bytes 12582920 | tf_op jit(solution)/shard_map/ppermute | solution.py:172
  470.2 16.9 %collective-permute-start.9 = (bf16[128,32,512]{2,1,0:T(8,128)(2,1)}, bf16[128,32,512]{2,1,0:T(8,128)(2,1)}, u32[]{:S(2)}, u32[]{:S(2)}) collective-permute-start(bf16[128,32,512]{2,1,0:T(8,128)(2,1)} %get-tuple-element.29.refs_9_), channel_id=1, source_target_pairs={{0,1},{1,0},{2,3},{3,2},{4,5},{5,4},{6,7},{7,6}} | collective-permute-start | bytes 12582920 | tf_op jit(solution)/shard_map/ppermute | solution.py:172
  637.6 152.5 %collective-permute-start.13 = (bf16[128,128,512]{2,1,0:T(8,128)(2,1)}, bf16[128,128,512]{2,1,0:T(8,128)(2,1)}, u32[]{:S(2)}, u32[]{:S(2)}) collective-permute-start(bf16[128,128,512]{2,1,0:T(8,128)(2,1)} %get-tuple-element.37.refs_5_), channel_id=1, source_target_pairs={{0,1},{1,0},{2,3},{3,2},{4,5},{5,4},{6,7},{7,6}} | collective-permute-start | bytes 50331656 | tf_op jit(solution)/shard_map/ppermute | solution.py:172
  740.6 49.5 %collective-permute-start.12 = (bf16[128,128,512]{2,1,0:T(8,128)(2,1)}, bf16[128,128,512]{2,1,0:T(8,128)(2,1)}, u32[]{:S(2)}, u32[]{:S(2)}) collective-permute-start(bf16[128,128,512]{2,1,0:T(8,128)(2,1)} %get-tuple-element.36.refs_4_), channel_id=1, source_target_pairs={{0,1},{1,0},{2,3},{3,2},{4,5},{5,4},{6,7},{7,6}} | collective-permute-start | bytes 50331656 | tf_op jit(solution)/shard_map/ppermute | solution.py:172
  740.6 37.5 %collective-permute-start.11 = (bf16[128,128,256]{2,1,0:T(8,128)(2,1)}, bf16[128,128,256]{2,1,0:T(8,128)(2,1)}, u32[]{:S(2)}, u32[]{:S(2)}) collective-permute-start(bf16[128,128,256]{2,1,0:T(8,128)(2,1)} %get-tuple-element.35), channel_id=1, source_target_pairs={{0,1},{1,0},{2,3},{3,2},{4,5},{5,4},{6,7},{7,6}} | collective-permute-start | bytes 25165832 | tf_op jit(solution)/shard_map/ppermute | solution.py:172
  741.1 49.0 %collective-permute-start.10 = (bf16[128,128,256]{2,1,0:T(8,128)(2,1)}, bf16[128,128,256]{2,1,0:T(8,128)(2,1)}, u32[]{:S(2)}, u32[]{:S(2)}) collective-permute-start(bf16[128,128,256]{2,1,0:T(8,128)(2,1)} %get-tuple-element.34), channel_id=1, source_target_pairs={{0,1},{1,0},{2,3},{3,2},{4,5},{5,4},{6,7},{7,6}} | collective-permute-start | bytes 25165832 | tf_op jit(solution)/shard_map/ppermute | solution.py:172
  857.5 125.0 %collective-permute-start.14 = (bf16[32,512,128]{2,1,0:T(8,128)(2,1)}, bf16[32,512,128]{2,1,0:T(8,128)(2,1)}, u32[]{:S(2)}, u32[]{:S(2)}) collective-permute-start(bf16[32,512,128]{2,1,0:T(8,128)(2,1)} %shard_map.117), channel_id=1, source_target_pairs={{0,2},{2,0},{1,3},{3,1},{4,6},{6,4},{5,7},{7,5}} | collective-permute-start | bytes 12582920 | tf_op jit(solution)/shard_map/ppermute | solution.py:169
  875.1 258.9 %collective-permute-start.16 = (bf16[32,512,128]{2,1,0:T(8,128)(2,1)}, bf16[32,512,128]{2,1,0:T(8,128)(2,1)}, u32[]{:S(2)}, u32[]{:S(2)}) collective-permute-start(bf16[32,512,128]{2,1,0:T(8,128)(2,1)} %shard_map.119), channel_id=1, source_target_pairs={{0,2},{2,0},{1,3},{3,1},{4,6},{6,4},{5,7},{7,5}} | collective-permute-start | bytes 12582920 | tf_op jit(solution)/shard_map/ppermute | solution.py:169
  875.7 255.4 %collective-permute-start.15 = (bf16[32,512,128]{2,1,0:T(8,128)(2,1)}, bf16[32,512,128]{2,1,0:T(8,128)(2,1)}, u32[]{:S(2)}, u32[]{:S(2)}) collective-permute-start(bf16[32,512,128]{2,1,0:T(8,128)(2,1)} %shard_map.118), channel_id=1, source_target_pairs={{0,2},{2,0},{1,3},{3,1},{4,6},{6,4},{5,7},{7,5}} | collective-permute-start | bytes 12582920 | tf_op jit(solution)/shard_map/ppermute | solution.py:169
  893.4 326.7 %collective-permute-start.17 = (bf16[32,512,128]{2,1,0:T(8,128)(2,1)}, bf16[32,512,128]{2,1,0:T(8,128)(2,1)}, u32[]{:S(2)}, u32[]{:S(2)}) collective-permute-start(bf16[32,512,128]{2,1,0:T(8,128)(2,1)} %shard_map.120), channel_id=1, source_target_pairs={{0,2},{2,0},{1,3},{3,1},{4,6},{6,4},{5,7},{7,5}} | collective-permute-start | bytes 12582920 | tf_op jit(solution)/shard_map/ppermute | solution.py:169
